TPU v7x, 32 devices: a whole 2x2x4 slice. The times are simulated.
32 devices in a mesh: rep: 4 (over x, core), row: 2 (over y), col: 4 (over z).
Axes of the slice: x: 2, y: 2, z: 4, core: 2. Of those that a mesh axis runs over, the one named last changes fastest.
Arguments:
- spin_init: bfloat16 [256, 8192], P('rep', 'row'), may hold values from -1 to 1, as said below
- couplings: bfloat16 [2, 4, 1024, 8192], P(None, 'col', None, 'row'), may hold values from -1 to 1, as said below
- flip_noise: float32 [10, 256, 8192], P(None, 'rep', 'row'), may hold values from 0 to 17, as said below
- colors: int32 [8192], P('row'), may hold values 0 or 1
- beta_steps: int32 [256], replicated, may hold values from 96 to 1024
- partners: int32 [256], replicated, may hold values from 0 to 255, as said below
- swap_noise: float32 [256], replicated, may hold values from 0 to 17, as said below
Outputs:
- spins_out: bfloat16 [256, 8192], P('rep', 'row')
- energies: float32 [256], P('rep')
Inputs may be any that keep to these rules, and one draw needn't show every extreme that they name: `spin_init`: every entry is -1 or +1. `couplings`: the 8192 x 8192 matrix is symmetric, zero on its diagonal, and every other entry is -1 or +1. `flip_noise`: independent exponential variates of mean one. `swap_noise`: independent exponential variates of mean one. Pairs slots: partners[partners[r]] = r and partners[r] != r for every slot.
All inputs are finite; a program needn't handle non-finite values. No bound on the sum of `colors` on one device may be relied on, other than what follows from the above.
Results may differ from a plain program's by a relative error of at most 0.001.
Values may be sent and summed in bfloat16 or wider, within the bound.
A program may use at most 64 MiB of HBM per device.

v0:
```python
import math
import jax
import jax.numpy as jnp
from jax import lax
from jax.sharding import PartitionSpec as P

N = 8192
SWEEPS = 10


def metropolis(spin_state, fields, parity, color_part, noise_part, beta_col):
    values = spin_state.astype(jnp.float32)
    energy_cost = beta_col * (values * fields) * (1.0 / 16384.0)
    flipped = (color_part == parity)[None, :] & (energy_cost < noise_part)
    return jnp.where(flipped, -values, values).astype(jnp.bfloat16)


def partial_fields(strided, coupling_block):
    return jnp.dot(strided, coupling_block, preferred_element_type=jnp.float32)


def per_device(spin_init, couplings, flip_noise, colors, beta_steps, partners, swap_noise):
    rep_dev, row_width = spin_init.shape
    col_count = lax.axis_size("col")
    col_index = lax.axis_index("col")
    rep_index = lax.axis_index("rep")
    piece_size = row_width // col_count
    coupling_block = couplings.reshape(-1, row_width)
    beta_col = lax.dynamic_slice_in_dim(beta_steps, rep_index * rep_dev, rep_dev).astype(
        jnp.float32
    )[:, None]
    color_part = lax.dynamic_slice_in_dim(colors, col_index * piece_size, piece_size)
    noise_part = lax.dynamic_slice_in_dim(flip_noise, col_index * piece_size, piece_size, 2)

    def strided_of(spin_state):
        return lax.all_gather(spin_state, "row", axis=1, tiled=True)

    def one_sweep(step_index, spin_state):
        terms = partial_fields(strided_of(spin_state), coupling_block)
        fields = lax.psum_scatter(terms, "col", scatter_dimension=1, tiled=True)
        return metropolis(
            spin_state, fields, step_index % 2, color_part, noise_part[step_index], beta_col
        )

    start_pieces = lax.dynamic_slice_in_dim(spin_init, col_index * piece_size, piece_size, 1)
    final_pieces = lax.fori_loop(0, SWEEPS, one_sweep, start_pieces)
    strided = strided_of(final_pieces)
    final_rows = lax.all_gather(final_pieces, "col", axis=1, tiled=True)
    every_spins = lax.all_gather(final_rows, "rep", axis=0, tiled=True)
    final_partial = partial_fields(strided, coupling_block)
    row_values = final_rows.astype(jnp.float32)
    final_local = lax.psum(final_partial, "col")
    total_sum = lax.psum(jnp.sum(row_values * final_local, axis=1), "row")
    energy = -0.5 * total_sum
    every_energy = lax.all_gather(energy, "rep", axis=0, tiled=True)
    slot_ids = rep_index * rep_dev + jnp.arange(rep_dev, dtype=jnp.int32)
    mate_ids = lax.dynamic_slice_in_dim(partners, rep_index * rep_dev, rep_dev)
    all_betas = beta_steps.astype(jnp.float32)
    mate_energy = every_energy[mate_ids]
    swap_gain = (
        (beta_col[:, 0] - all_betas[mate_ids])
        * (energy - mate_energy)
        * (1.0 / (64.0 * N * math.sqrt(N)))
    )
    accept = swap_gain + swap_noise[jnp.minimum(slot_ids, mate_ids)] > 0.0
    spins_out = jnp.where(accept[:, None], every_spins[mate_ids], final_rows)
    energies = jnp.where(accept, mate_energy, energy) * (1.0 / (N * math.sqrt(N)))
    return (spins_out, energies)


def solution(mesh):
    in_specs = (
        P("rep", "row"),
        P(None, "col", None, "row"),
        P(None, "rep", "row"),
        P("row"),
        P(),
        P(),
        P(),
    )
    out_specs = (P("rep", "row"), P("rep"))
    return jax.shard_map(
        per_device, mesh=mesh, in_specs=in_specs, out_specs=out_specs, check_vma=False
    )
```

profile of v0, /device:TPU:0, one launch (start us, length us, event | category | flops | bytes accessed | tf_op | source)
XLA Modules:
  0.0 540.9 jit_solution(17251068194962414624)
XLA Ops:
  12.4 431.6 %while.15 = (s32[]{:T(128)}, bf16[64,1024]{1,0:T(8,128)(2,1)S(1)}, s32[1024]{0:T(1024)S(1)}, f32[64,1]{0,1:T(1,128)S(1)}, bf16[2048,4096]{1,0:T(8,128)(2,1)}, /*...) while((s32[]{:T(128)}, bf16[64,1024]{1,0:T(8,128)(2,1)S(1)}, s32[1024]{0:T(1024)S(1)}, ...), condition=%wide.region_2.3_spmd, body=%wide.region_0.2_spmd.sunk | while | flops 1074332672 | bytes 23206348 | solution.py:46
  19.6 9.8 %fusion.17 = f32[64,4096]{1,0:T(8,128)} fusion(bf16[64,2048]{1,0:T(8,128)(2,1)S(1)} %all_gather.27, bf16[2048,4096]{1,0:T(8,128)(2,1)} %get-tuple-element.233), kind=kOutput, calls=%fused_computation.24.clone.1 | convolution fusion | flops 1073741824 | bytes 18087936 | tf_op jit(solution)/shard_map/while/body/eval_jaxpr/dot_general | solution.py:19
  29.4 28.9 %reduce-scatter.2.cloned.1.call-done = f32[64,1024]{1,0:T(8,128)} async-done(((f32[64,4096]{1,0:T(8,128)}), f32[64,1024]{1,0:T(8,128)}) %reduce-scatter.2.cloned.1.call-update) | async-done | bytes 262160 | tf_op jit(solution)/shard_map/while/body/eval_jaxpr/reduce_scatter | solution.py:40
  65.1 9.8 %fusion.17 = f32[64,4096]{1,0:T(8,128)} fusion(bf16[64,2048]{1,0:T(8,128)(2,1)S(1)} %all_gather.27, bf16[2048,4096]{1,0:T(8,128)(2,1)} %get-tuple-element.233), kind=kOutput, calls=%fused_computation.24.clone.1 | convolution fusion | flops 1073741824 | bytes 18087936 | tf_op jit(solution)/shard_map/while/body/eval_jaxpr/dot_general | solution.py:19
  74.9 26.1 %reduce-scatter.2.cloned.1.call-done = f32[64,1024]{1,0:T(8,128)} async-done(((f32[64,4096]{1,0:T(8,128)}), f32[64,1024]{1,0:T(8,128)}) %reduce-scatter.2.cloned.1.call-update) | async-done | bytes 262160 | tf_op jit(solution)/shard_map/while/body/eval_jaxpr/reduce_scatter | solution.py:40
  107.8 9.8 %fusion.17 = f32[64,4096]{1,0:T(8,128)} fusion(bf16[64,2048]{1,0:T(8,128)(2,1)S(1)} %all_gather.27, bf16[2048,4096]{1,0:T(8,128)(2,1)} %get-tuple-element.233), kind=kOutput, calls=%fused_computation.24.clone.1 | convolution fusion | flops 1073741824 | bytes 18087936 | tf_op jit(solution)/shard_map/while/body/eval_jaxpr/dot_general | solution.py:19
  117.6 26.1 %reduce-scatter.2.cloned.1.call-done = f32[64,1024]{1,0:T(8,128)} async-done(((f32[64,4096]{1,0:T(8,128)}), f32[64,1024]{1,0:T(8,128)}) %reduce-scatter.2.cloned.1.call-update) | async-done | bytes 262160 | tf_op jit(solution)/shard_map/while/body/eval_jaxpr/reduce_scatter | solution.py:40
  150.5 9.8 %fusion.17 = f32[64,4096]{1,0:T(8,128)} fusion(bf16[64,2048]{1,0:T(8,128)(2,1)S(1)} %all_gather.27, bf16[2048,4096]{1,0:T(8,128)(2,1)} %get-tuple-element.233), kind=kOutput, calls=%fused_computation.24.clone.1 | convolution fusion | flops 1073741824 | bytes 18087936 | tf_op jit(solution)/shard_map/while/body/eval_jaxpr/dot_general | solution.py:19
  160.4 26.2 %reduce-scatter.2.cloned.1.call-done = f32[64,1024]{1,0:T(8,128)} async-done(((f32[64,4096]{1,0:T(8,128)}), f32[64,1024]{1,0:T(8,128)}) %reduce-scatter.2.cloned.1.call-update) | async-done | bytes 262160 | tf_op jit(solution)/shard_map/while/body/eval_jaxpr/reduce_scatter | solution.py:40
  193.3 9.8 %fusion.17 = f32[64,4096]{1,0:T(8,128)} fusion(bf16[64,2048]{1,0:T(8,128)(2,1)S(1)} %all_gather.27, bf16[2048,4096]{1,0:T(8,128)(2,1)} %get-tuple-element.233), kind=kOutput, calls=%fused_computation.24.clone.1 | convolution fusion | flops 1073741824 | bytes 18087936 | tf_op jit(solution)/shard_map/while/body/eval_jaxpr/dot_general | solution.py:19
  203.1 26.1 %reduce-scatter.2.cloned.1.call-done = f32[64,1024]{1,0:T(8,128)} async-done(((f32[64,4096]{1,0:T(8,128)}), f32[64,1024]{1,0:T(8,128)}) %reduce-scatter.2.cloned.1.call-update) | async-done | bytes 262160 | tf_op jit(solution)/shard_map/while/body/eval_jaxpr/reduce_scatter | solution.py:40
  236.0 9.8 %fusion.17 = f32[64,4096]{1,0:T(8,128)} fusion(bf16[64,2048]{1,0:T(8,128)(2,1)S(1)} %all_gather.27, bf16[2048,4096]{1,0:T(8,128)(2,1)} %get-tuple-element.233), kind=kOutput, calls=%fused_computation.24.clone.1 | convolution fusion | flops 1073741824 | bytes 18087936 | tf_op jit(solution)/shard_map/while/body/eval_jaxpr/dot_general | solution.py:19
  245.8 26.1 %reduce-scatter.2.cloned.1.call-done = f32[64,1024]{1,0:T(8,128)} async-done(((f32[64,4096]{1,0:T(8,128)}), f32[64,1024]{1,0:T(8,128)}) %reduce-scatter.2.cloned.1.call-update) | async-done | bytes 262160 | tf_op jit(solution)/shard_map/while/body/eval_jaxpr/reduce_scatter | solution.py:40
  278.8 9.8 %fusion.17 = f32[64,4096]{1,0:T(8,128)} fusion(bf16[64,2048]{1,0:T(8,128)(2,1)S(1)} %all_gather.27, bf16[2048,4096]{1,0:T(8,128)(2,1)} %get-tuple-element.233), kind=kOutput, calls=%fused_computation.24.clone.1 | convolution fusion | flops 1073741824 | bytes 18087936 | tf_op jit(solution)/shard_map/while/body/eval_jaxpr/dot_general | solution.py:19
  288.6 26.1 %reduce-scatter.2.cloned.1.call-done = f32[64,1024]{1,0:T(8,128)} async-done(((f32[64,4096]{1,0:T(8,128)}), f32[64,1024]{1,0:T(8,128)}) %reduce-scatter.2.cloned.1.call-update) | async-done | bytes 262160 | tf_op jit(solution)/shard_map/while/body/eval_jaxpr/reduce_scatter | solution.py:40
  321.5 9.8 %fusion.17 = f32[64,4096]{1,0:T(8,128)} fusion(bf16[64,2048]{1,0:T(8,128)(2,1)S(1)} %all_gather.27, bf16[2048,4096]{1,0:T(8,128)(2,1)} %get-tuple-element.233), kind=kOutput, calls=%fused_computation.24.clone.1 | convolution fusion | flops 1073741824 | bytes 18087936 | tf_op jit(solution)/shard_map/while/body/eval_jaxpr/dot_general | solution.py:19
  331.3 26.1 %reduce-scatter.2.cloned.1.call-done = f32[64,1024]{1,0:T(8,128)} async-done(((f32[64,4096]{1,0:T(8,128)}), f32[64,1024]{1,0:T(8,128)}) %reduce-scatter.2.cloned.1.call-update) | async-done | bytes 262160 | tf_op jit(solution)/shard_map/while/body/eval_jaxpr/reduce_scatter | solution.py:40
  364.3 9.8 %fusion.17 = f32[64,4096]{1,0:T(8,128)} fusion(bf16[64,2048]{1,0:T(8,128)(2,1)S(1)} %all_gather.27, bf16[2048,4096]{1,0:T(8,128)(2,1)} %get-tuple-element.233), kind=kOutput, calls=%fused_computation.24.clone.1 | convolution fusion | flops 1073741824 | bytes 18087936 | tf_op jit(solution)/shard_map/while/body/eval_jaxpr/dot_general | solution.py:19
  374.1 26.1 %reduce-scatter.2.cloned.1.call-done = f32[64,1024]{1,0:T(8,128)} async-done(((f32[64,4096]{1,0:T(8,128)}), f32[64,1024]{1,0:T(8,128)}) %reduce-scatter.2.cloned.1.call-update) | async-done | bytes 262160 | tf_op jit(solution)/shard_map/while/body/eval_jaxpr/reduce_scatter | solution.py:40
  407.0 9.8 %fusion.17 = f32[64,4096]{1,0:T(8,128)} fusion(bf16[64,2048]{1,0:T(8,128)(2,1)S(1)} %all_gather.27, bf16[2048,4096]{1,0:T(8,128)(2,1)} %get-tuple-element.233), kind=kOutput, calls=%fused_computation.24.clone.1 | convolution fusion | flops 1073741824 | bytes 18087936 | tf_op jit(solution)/shard_map/while/body/eval_jaxpr/dot_general | solution.py:19
  416.8 26.1 %reduce-scatter.2.cloned.1.call-done = f32[64,1024]{1,0:T(8,128)} async-done(((f32[64,4096]{1,0:T(8,128)}), f32[64,1024]{1,0:T(8,128)}) %reduce-scatter.2.cloned.1.call-update) | async-done | bytes 262160 | tf_op jit(solution)/shard_map/while/body/eval_jaxpr/reduce_scatter | solution.py:40
  449.8 9.8 %fusion.6 = f32[64,4096]{1,0:T(8,128)} fusion(bf16[64,2048]{1,0:T(8,128)(2,1)S(1)} %all_gather.23, bf16[2048,4096]{1,0:T(8,128)(2,1)} %get-tuple-element.241), kind=kOutput, calls=%fused_computation.25 | convolution fusion | flops 1073741824 | bytes 18087936 | tf_op jit(solution)/shard_map/dot_general | solution.py:19
  459.7 20.4 %all_gather.22 = bf16[64,4096]{1,0:T(8,128)(2,1)} all-gather(bf16[64,1024]{1,0:T(8,128)(2,1)S(1)} %get-tuple-element.157), channel_id=1, replica_groups=mesh['rep'=4,'row'=2,'col'=4] {'col'}, dimensions={1}, use_global_device_ids=true | all-gather | bytes 655360 | tf_op jit(solution)/shard_map/all_gather | solution.py:48
  483.0 32.0 %all-reduce.3.cloned.1.call-done = f32[64,4096]{1,0:T(8,128)} async-done(((f32[64,4096]{1,0:T(8,128)}), f32[64,4096]{1,0:T(8,128)}) %all-reduce.3.cloned.1.call-update) | async-done | bytes 1048592 | tf_op jit(solution)/shard_map/psum | solution.py:52
  (86 shorter events, 100.6 us)
Async XLA Ops:
  8.0 1.0 copy-start
  12.4 45.9 %reduce-scatter.2.cloned.1.call-start = ((), (), s32[]{:S(2)}) async-start(), calls=%async_computation.3 | async-start | bytes 1310720 | tf_op jit(solution)/shard_map/while/body/eval_jaxpr/reduce_scatter | solution.py:40
  59.4 41.6 %reduce-scatter.2.cloned.1.call-start = ((), (), s32[]{:S(2)}) async-start(), calls=%async_computation.3 | async-start | bytes 1310720 | tf_op jit(solution)/shard_map/while/body/eval_jaxpr/reduce_scatter | solution.py:40
  102.1 41.6 %reduce-scatter.2.cloned.1.call-start = ((), (), s32[]{:S(2)}) async-start(), calls=%async_computation.3 | async-start | bytes 1310720 | tf_op jit(solution)/shard_map/while/body/eval_jaxpr/reduce_scatter | solution.py:40
  144.9 41.7 %reduce-scatter.2.cloned.1.call-start = ((), (), s32[]{:S(2)}) async-start(), calls=%async_computation.3 | async-start | bytes 1310720 | tf_op jit(solution)/shard_map/while/body/eval_jaxpr/reduce_scatter | solution.py:40
  187.6 41.6 %reduce-scatter.2.cloned.1.call-start = ((), (), s32[]{:S(2)}) async-start(), calls=%async_computation.3 | async-start | bytes 1310720 | tf_op jit(solution)/shard_map/while/body/eval_jaxpr/reduce_scatter | solution.py:40
  230.3 41.6 %reduce-scatter.2.cloned.1.call-start = ((), (), s32[]{:S(2)}) async-start(), calls=%async_computation.3 | async-start | bytes 1310720 | tf_op jit(solution)/shard_map/while/body/eval_jaxpr/reduce_scatter | solution.py:40
  273.1 41.6 %reduce-scatter.2.cloned.1.call-start = ((), (), s32[]{:S(2)}) async-start(), calls=%async_computation.3 | async-start | bytes 1310720 | tf_op jit(solution)/shard_map/while/body/eval_jaxpr/reduce_scatter | solution.py:40
  315.8 41.6 %reduce-scatter.2.cloned.1.call-start = ((), (), s32[]{:S(2)}) async-start(), calls=%async_computation.3 | async-start | bytes 1310720 | tf_op jit(solution)/shard_map/while/body/eval_jaxpr/reduce_scatter | solution.py:40
  358.6 41.6 %reduce-scatter.2.cloned.1.call-start = ((), (), s32[]{:S(2)}) async-start(), calls=%async_computation.3 | async-start | bytes 1310720 | tf_op jit(solution)/shard_map/while/body/eval_jaxpr/reduce_scatter | solution.py:40
  401.3 41.6 %reduce-scatter.2.cloned.1.call-start = ((), (), s32[]{:S(2)}) async-start(), calls=%async_computation.3 | async-start | bytes 1310720 | tf_op jit(solution)/shard_map/while/body/eval_jaxpr/reduce_scatter | solution.py:40
  444.1 36.0 %copy-start.2 = (s32[256]{0:T(256)S(1)}, s32[256]{0:T(256)}, u32[]{:S(2)}) copy-start(s32[256]{0:T(256)} %param.13) | copy-start | bytes 3076
  444.1 36.0 %copy-start.4 = (u32[32]{0:T(128)S(1)}, u32[32]{0:T(128)}, u32[]{:S(2)}) copy-start(u32[32]{0:T(128)} %constant.92) | copy-start | bytes 388
  444.1 37.2 %copy-start.3 = (s32[256]{0:T(256)S(1)}, s32[256]{0:T(256)}, u32[]{:S(2)}) copy-start(s32[256]{0:T(256)} %param.14) | copy-start | bytes 3076
  444.1 37.3 %copy-start.1 = (f32[256]{0:T(256)S(1)}, f32[256]{0:T(256)}, u32[]{:S(2)}) copy-start(f32[256]{0:T(256)} %param.15) | copy-start | bytes 3076
  444.1 70.9 %all-reduce.3.cloned.1.call-start = ((), (), s32[]{:S(2)}) async-start(), calls=%async_computation.1 | async-start | bytes 2097152 | tf_op jit(solution)/shard_map/psum | solution.py:52
  459.6 69.0 %all-gather.2.cloned.1.call-start = ((), (), s32[]{:S(2)}) async-start(), calls=%async_computation.2 | async-start | bytes 2621440 | tf_op jit(solution)/shard_map/all_gather | solution.py:49
Sparse Core Ops, SparseCore 0:
  29.5 28.7 reduce-scatter.1
  75.0 25.9 reduce-scatter.1
  117.7 25.9 reduce-scatter.1
  160.5 26.0 reduce-scatter.1
  203.2 25.9 reduce-scatter.1
  246.0 25.9 reduce-scatter.1
  288.7 25.9 reduce-scatter.1
  331.4 25.9 reduce-scatter.1
  374.2 25.9 reduce-scatter.1
  416.9 25.9 reduce-scatter.1
  480.2 21.6 all-gather.1
Sparse Core Ops, SparseCore 1:
  459.7 55.3 all-reduce.2
where the time goes:
time: 542 us; the launch traced here: 541 us
  waiting for transfers between devices  296 us (55%)
  matrix products  107 us (20%)
  blocking collectives  94.4 us (17%)
  other arithmetic  16 us (3%)
  between operations  15.9 us (3%)
  local copies, waits for them, and re-layouts  9.87 us (2%)
    reduce_scatter x10, waiting for transfers between devices, one_sweep(): fields = lax.psum_scatter(terms, 'col', scatter_dimension=1, tiled=True)  264 us
    dot_general x11, matrix products, partial_fields(): return jnp.dot(strided, coupling_block, preferred_element_type=jnp.float32)  107 us
    all_gather x11, blocking collectives, strided_of(): return lax.all_gather(spin_state, 'row', axis=1, tiled=True)  63.5 us
    psum x1, waiting for transfers between devices, per_device(): final_local = lax.psum(final_partial, 'col')  32 us
    all_gather x1, blocking collectives, per_device(): final_rows = lax.all_gather(final_pieces, 'col', axis=1, tiled=True)  20.4 us
    convert_element_type x10, other arithmetic, metropolis(): return jnp.where(flipped, -values, values).astype(jnp.bfloat16)  10.9 us
  transfers between devices with their start and end apart: 12, of which 11 were waited for; matrix products, arithmetic and copies ran while one was open for 1% of the time, Pallas kernels for 0%

commit v1 on v0

--- a/solution.py
+++ b/solution.py
@@ -33,7 +33,9 @@
     noise_part = lax.dynamic_slice_in_dim(flip_noise, col_index * piece_size, piece_size, 2)
 
     def strided_of(spin_state):
-        return lax.all_gather(spin_state, "row", axis=1, tiled=True)
+        return jnp.concatenate(
+            lax.all_to_all(jnp.stack([spin_state] * lax.axis_size("row")), "row", 0, 0), axis=1
+        )
 
     def one_sweep(step_index, spin_state):
         terms = partial_fields(strided_of(spin_state), coupling_block)

time: 542 us -> 554 us (1.022)
  blocking collectives: 94.4 us -> 117 us
  waiting for transfers between devices: 296 us -> 285 us
    all_to_all x0 -> x11, blocking collectives: none -> 86.3 us  [strided_of(): lax.all_to_all(jnp.stack([spin_state] * lax.axis_size('row')), 'row', 0, 0)]
    all_gather x11 -> x0, blocking collectives: 63.5 us -> none  [strided_of(): return lax.all_gather(spin_state, 'row', axis=1, tiled=True)]
    reduce_scatter x10, waiting for transfers between devices: 264 us -> 254 us  [one_sweep(): fields = lax.psum_scatter(terms, 'col', scatter_dimension=1, tiled=True)]
where the time goes in v1:
time: 554 us; the launch traced here: 553 us
  waiting for transfers between devices  285 us (51%)
  blocking collectives  117 us (21%)
  matrix products  107 us (19%)
  other arithmetic  16.2 us (3%)
  between operations  15.9 us (3%)
  local copies, waits for them, and re-layouts  10.1 us (2%)
    reduce_scatter x10, waiting for transfers between devices, one_sweep(): fields = lax.psum_scatter(terms, 'col', scatter_dimension=1, tiled=True)  254 us
    dot_general x11, matrix products, partial_fields(): return jnp.dot(strided, coupling_block, preferred_element_type=jnp.float32)  107 us
    all_to_all x11, blocking collectives, strided_of(): lax.all_to_all(jnp.stack([spin_state] * lax.axis_size('row')), 'row', 0, 0)  86.3 us
    psum x1, waiting for transfers between devices, per_device(): final_local = lax.psum(final_partial, 'col')  30.9 us
    all_gather x1, blocking collectives, per_device(): final_rows = lax.all_gather(final_pieces, 'col', axis=1, tiled=True)  20.3 us
  transfers between devices with their start and end apart: 12, of which 11 were waited for; matrix products, arithmetic and copies ran while one was open for 1% of the time, Pallas kernels for 0%

profile of v1, /device:TPU:0, one launch (start us, length us, event | category | flops | bytes accessed | tf_op | source)
XLA Modules:
  0.0 552.6 jit_solution(15252093343678648281)
XLA Ops:
  12.4 442.3 %while.15 = (s32[]{:T(128)}, bf16[64,1024]{1,0:T(8,128)(2,1)S(1)}, s32[1024]{0:T(1024)S(1)}, f32[64,1]{0,1:T(1,128)S(1)}, bf16[2048,4096]{1,0:T(8,128)(2,1)}, /*...) while((s32[]{:T(128)}, bf16[64,1024]{1,0:T(8,128)(2,1)S(1)}, s32[1024]{0:T(1024)S(1)}, ...), condition=%wide.region_2.3_spmd, body=%wide.region_0.2_spmd.sunk | while | flops 1074463744 | bytes 24254924 | solution.py:48
  21.7 9.8 %fusion.17 = f32[64,4096]{1,0:T(8,128)} fusion(bf16[64,2048]{1,0:T(8,128)(2,1)S(1)} %bitcast.36, bf16[2048,4096]{1,0:T(8,128)(2,1)} %get-tuple-element.233), kind=kOutput, calls=%fused_computation.26.clone.1 | convolution fusion | flops 1073741824 | bytes 18087936 | tf_op jit(solution)/shard_map/while/body/eval_jaxpr/dot_general | solution.py:19
  31.5 27.8 %reduce-scatter.2.cloned.1.call-done = f32[64,1024]{1,0:T(8,128)} async-done(((f32[64,4096]{1,0:T(8,128)}), f32[64,1024]{1,0:T(8,128)}) %reduce-scatter.2.cloned.1.call-update) | async-done | bytes 262160 | tf_op jit(solution)/shard_map/while/body/eval_jaxpr/reduce_scatter | solution.py:42
  68.2 9.8 %fusion.17 = f32[64,4096]{1,0:T(8,128)} fusion(bf16[64,2048]{1,0:T(8,128)(2,1)S(1)} %bitcast.36, bf16[2048,4096]{1,0:T(8,128)(2,1)} %get-tuple-element.233), kind=kOutput, calls=%fused_computation.26.clone.1 | convolution fusion | flops 1073741824 | bytes 18087936 | tf_op jit(solution)/shard_map/while/body/eval_jaxpr/dot_general | solution.py:19
  78.1 25.1 %reduce-scatter.2.cloned.1.call-done = f32[64,1024]{1,0:T(8,128)} async-done(((f32[64,4096]{1,0:T(8,128)}), f32[64,1024]{1,0:T(8,128)}) %reduce-scatter.2.cloned.1.call-update) | async-done | bytes 262160 | tf_op jit(solution)/shard_map/while/body/eval_jaxpr/reduce_scatter | solution.py:42
  112.1 9.8 %fusion.17 = f32[64,4096]{1,0:T(8,128)} fusion(bf16[64,2048]{1,0:T(8,128)(2,1)S(1)} %bitcast.36, bf16[2048,4096]{1,0:T(8,128)(2,1)} %get-tuple-element.233), kind=kOutput, calls=%fused_computation.26.clone.1 | convolution fusion | flops 1073741824 | bytes 18087936 | tf_op jit(solution)/shard_map/while/body/eval_jaxpr/dot_general | solution.py:19
  121.9 25.1 %reduce-scatter.2.cloned.1.call-done = f32[64,1024]{1,0:T(8,128)} async-done(((f32[64,4096]{1,0:T(8,128)}), f32[64,1024]{1,0:T(8,128)}) %reduce-scatter.2.cloned.1.call-update) | async-done | bytes 262160 | tf_op jit(solution)/shard_map/while/body/eval_jaxpr/reduce_scatter | solution.py:42
  155.9 9.8 %fusion.17 = f32[64,4096]{1,0:T(8,128)} fusion(bf16[64,2048]{1,0:T(8,128)(2,1)S(1)} %bitcast.36, bf16[2048,4096]{1,0:T(8,128)(2,1)} %get-tuple-element.233), kind=kOutput, calls=%fused_computation.26.clone.1 | convolution fusion | flops 1073741824 | bytes 18087936 | tf_op jit(solution)/shard_map/while/body/eval_jaxpr/dot_general | solution.py:19
  165.7 25.1 %reduce-scatter.2.cloned.1.call-done = f32[64,1024]{1,0:T(8,128)} async-done(((f32[64,4096]{1,0:T(8,128)}), f32[64,1024]{1,0:T(8,128)}) %reduce-scatter.2.cloned.1.call-update) | async-done | bytes 262160 | tf_op jit(solution)/shard_map/while/body/eval_jaxpr/reduce_scatter | solution.py:42
  199.7 9.8 %fusion.17 = f32[64,4096]{1,0:T(8,128)} fusion(bf16[64,2048]{1,0:T(8,128)(2,1)S(1)} %bitcast.36, bf16[2048,4096]{1,0:T(8,128)(2,1)} %get-tuple-element.233), kind=kOutput, calls=%fused_computation.26.clone.1 | convolution fusion | flops 1073741824 | bytes 18087936 | tf_op jit(solution)/shard_map/while/body/eval_jaxpr/dot_general | solution.py:19
  209.5 25.1 %reduce-scatter.2.cloned.1.call-done = f32[64,1024]{1,0:T(8,128)} async-done(((f32[64,4096]{1,0:T(8,128)}), f32[64,1024]{1,0:T(8,128)}) %reduce-scatter.2.cloned.1.call-update) | async-done | bytes 262160 | tf_op jit(solution)/shard_map/while/body/eval_jaxpr/reduce_scatter | solution.py:42
  243.5 9.8 %fusion.17 = f32[64,4096]{1,0:T(8,128)} fusion(bf16[64,2048]{1,0:T(8,128)(2,1)S(1)} %bitcast.36, bf16[2048,4096]{1,0:T(8,128)(2,1)} %get-tuple-element.233), kind=kOutput, calls=%fused_computation.26.clone.1 | convolution fusion | flops 1073741824 | bytes 18087936 | tf_op jit(solution)/shard_map/while/body/eval_jaxpr/dot_general | solution.py:19
  253.3 25.1 %reduce-scatter.2.cloned.1.call-done = f32[64,1024]{1,0:T(8,128)} async-done(((f32[64,4096]{1,0:T(8,128)}), f32[64,1024]{1,0:T(8,128)}) %reduce-scatter.2.cloned.1.call-update) | async-done | bytes 262160 | tf_op jit(solution)/shard_map/while/body/eval_jaxpr/reduce_scatter | solution.py:42
  287.3 9.8 %fusion.17 = f32[64,4096]{1,0:T(8,128)} fusion(bf16[64,2048]{1,0:T(8,128)(2,1)S(1)} %bitcast.36, bf16[2048,4096]{1,0:T(8,128)(2,1)} %get-tuple-element.233), kind=kOutput, calls=%fused_computation.26.clone.1 | convolution fusion | flops 1073741824 | bytes 18087936 | tf_op jit(solution)/shard_map/while/body/eval_jaxpr/dot_general | solution.py:19
  297.1 25.1 %reduce-scatter.2.cloned.1.call-done = f32[64,1024]{1,0:T(8,128)} async-done(((f32[64,4096]{1,0:T(8,128)}), f32[64,1024]{1,0:T(8,128)}) %reduce-scatter.2.cloned.1.call-update) | async-done | bytes 262160 | tf_op jit(solution)/shard_map/while/body/eval_jaxpr/reduce_scatter | solution.py:42
  331.1 9.8 %fusion.17 = f32[64,4096]{1,0:T(8,128)} fusion(bf16[64,2048]{1,0:T(8,128)(2,1)S(1)} %bitcast.36, bf16[2048,4096]{1,0:T(8,128)(2,1)} %get-tuple-element.233), kind=kOutput, calls=%fused_computation.26.clone.1 | convolution fusion | flops 1073741824 | bytes 18087936 | tf_op jit(solution)/shard_map/while/body/eval_jaxpr/dot_general | solution.py:19
  340.9 25.1 %reduce-scatter.2.cloned.1.call-done = f32[64,1024]{1,0:T(8,128)} async-done(((f32[64,4096]{1,0:T(8,128)}), f32[64,1024]{1,0:T(8,128)}) %reduce-scatter.2.cloned.1.call-update) | async-done | bytes 262160 | tf_op jit(solution)/shard_map/while/body/eval_jaxpr/reduce_scatter | solution.py:42
  374.9 9.8 %fusion.17 = f32[64,4096]{1,0:T(8,128)} fusion(bf16[64,2048]{1,0:T(8,128)(2,1)S(1)} %bitcast.36, bf16[2048,4096]{1,0:T(8,128)(2,1)} %get-tuple-element.233), kind=kOutput, calls=%fused_computation.26.clone.1 | convolution fusion | flops 1073741824 | bytes 18087936 | tf_op jit(solution)/shard_map/while/body/eval_jaxpr/dot_general | solution.py:19
  384.7 25.1 %reduce-scatter.2.cloned.1.call-done = f32[64,1024]{1,0:T(8,128)} async-done(((f32[64,4096]{1,0:T(8,128)}), f32[64,1024]{1,0:T(8,128)}) %reduce-scatter.2.cloned.1.call-update) | async-done | bytes 262160 | tf_op jit(solution)/shard_map/while/body/eval_jaxpr/reduce_scatter | solution.py:42
  418.7 9.8 %fusion.17 = f32[64,4096]{1,0:T(8,128)} fusion(bf16[64,2048]{1,0:T(8,128)(2,1)S(1)} %bitcast.36, bf16[2048,4096]{1,0:T(8,128)(2,1)} %get-tuple-element.233), kind=kOutput, calls=%fused_computation.26.clone.1 | convolution fusion | flops 1073741824 | bytes 18087936 | tf_op jit(solution)/shard_map/while/body/eval_jaxpr/dot_general | solution.py:19
  428.6 25.1 %reduce-scatter.2.cloned.1.call-done = f32[64,1024]{1,0:T(8,128)} async-done(((f32[64,4096]{1,0:T(8,128)}), f32[64,1024]{1,0:T(8,128)}) %reduce-scatter.2.cloned.1.call-update) | async-done | bytes 262160 | tf_op jit(solution)/shard_map/while/body/eval_jaxpr/reduce_scatter | solution.py:42
  462.6 9.8 %fusion.6 = f32[64,4096]{1,0:T(8,128)} fusion(bf16[64,2048]{1,0:T(8,128)(2,1)S(1)} %bitcast.40, bf16[2048,4096]{1,0:T(8,128)(2,1)} %get-tuple-element.241), kind=kOutput, calls=%fused_computation.27 | convolution fusion | flops 1073741824 | bytes 18087936 | tf_op jit(solution)/shard_map/dot_general | solution.py:19
  472.5 20.3 %all_gather.9 = bf16[64,4096]{1,0:T(8,128)(2,1)} all-gather(bf16[64,1024]{1,0:T(8,128)(2,1)S(1)} %get-tuple-element.157), channel_id=1, replica_groups=mesh['rep'=4,'row'=2,'col'=4] {'col'}, dimensions={1}, use_global_device_ids=true | all-gather | bytes 655360 | tf_op jit(solution)/shard_map/all_gather | solution.py:50
  495.7 30.9 %all-reduce.3.cloned.1.call-done = f32[64,4096]{1,0:T(8,128)} async-done(((f32[64,4096]{1,0:T(8,128)}), f32[64,4096]{1,0:T(8,128)}) %all-reduce.3.cloned.1.call-update) | async-done | bytes 1048592 | tf_op jit(solution)/shard_map/psum | solution.py:54
  (108 shorter events, 123.9 us)
Async XLA Ops:
  8.0 1.0 copy-start
  12.4 46.9 %reduce-scatter.2.cloned.1.call-start = ((), (), s32[]{:S(2)}) async-start(), calls=%async_computation.5 | async-start | bytes 1310720 | tf_op jit(solution)/shard_map/while/body/eval_jaxpr/reduce_scatter | solution.py:42
  60.4 42.7 %reduce-scatter.2.cloned.1.call-start = ((), (), s32[]{:S(2)}) async-start(), calls=%async_computation.5 | async-start | bytes 1310720 | tf_op jit(solution)/shard_map/while/body/eval_jaxpr/reduce_scatter | solution.py:42
  104.2 42.7 %reduce-scatter.2.cloned.1.call-start = ((), (), s32[]{:S(2)}) async-start(), calls=%async_computation.5 | async-start | bytes 1310720 | tf_op jit(solution)/shard_map/while/body/eval_jaxpr/reduce_scatter | solution.py:42
  148.1 42.7 %reduce-scatter.2.cloned.1.call-start = ((), (), s32[]{:S(2)}) async-start(), calls=%async_computation.5 | async-start | bytes 1310720 | tf_op jit(solution)/shard_map/while/body/eval_jaxpr/reduce_scatter | solution.py:42
  191.9 42.7 %reduce-scatter.2.cloned.1.call-start = ((), (), s32[]{:S(2)}) async-start(), calls=%async_computation.5 | async-start | bytes 1310720 | tf_op jit(solution)/shard_map/while/body/eval_jaxpr/reduce_scatter | solution.py:42
  235.7 42.7 %reduce-scatter.2.cloned.1.call-start = ((), (), s32[]{:S(2)}) async-start(), calls=%async_computation.5 | async-start | bytes 1310720 | tf_op jit(solution)/shard_map/while/body/eval_jaxpr/reduce_scatter | solution.py:42
  279.5 42.7 %reduce-scatter.2.cloned.1.call-start = ((), (), s32[]{:S(2)}) async-start(), calls=%async_computation.5 | async-start | bytes 1310720 | tf_op jit(solution)/shard_map/while/body/eval_jaxpr/reduce_scatter | solution.py:42
  323.3 42.7 %reduce-scatter.2.cloned.1.call-start = ((), (), s32[]{:S(2)}) async-start(), calls=%async_computation.5 | async-start | bytes 1310720 | tf_op jit(solution)/shard_map/while/body/eval_jaxpr/reduce_scatter | solution.py:42
  367.1 42.7 %reduce-scatter.2.cloned.1.call-start = ((), (), s32[]{:S(2)}) async-start(), calls=%async_computation.5 | async-start | bytes 1310720 | tf_op jit(solution)/shard_map/while/body/eval_jaxpr/reduce_scatter | solution.py:42
  410.9 42.7 %reduce-scatter.2.cloned.1.call-start = ((), (), s32[]{:S(2)}) async-start(), calls=%async_computation.5 | async-start | bytes 1310720 | tf_op jit(solution)/shard_map/while/body/eval_jaxpr/reduce_scatter | solution.py:42
  454.8 38.0 %copy-start.2 = (s32[256]{0:T(256)S(1)}, s32[256]{0:T(256)}, u32[]{:S(2)}) copy-start(s32[256]{0:T(256)} %param.13) | copy-start | bytes 3076
  454.8 38.0 %copy-start.4 = (u32[32]{0:T(128)S(1)}, u32[32]{0:T(128)}, u32[]{:S(2)}) copy-start(u32[32]{0:T(128)} %constant.92) | copy-start | bytes 388
  454.8 39.2 %copy-start.3 = (s32[256]{0:T(256)S(1)}, s32[256]{0:T(256)}, u32[]{:S(2)}) copy-start(s32[256]{0:T(256)} %param.14) | copy-start | bytes 3076
  454.8 39.3 %copy-start.1 = (f32[256]{0:T(256)S(1)}, f32[256]{0:T(256)}, u32[]{:S(2)}) copy-start(f32[256]{0:T(256)} %param.15) | copy-start | bytes 3076
  454.8 71.8 %all-reduce.3.cloned.1.call-start = ((), (), s32[]{:S(2)}) async-start(), calls=%async_computation.3 | async-start | bytes 2097152 | tf_op jit(solution)/shard_map/psum | solution.py:54
  472.4 67.9 %all-gather.2.cloned.1.call-start = ((), (), s32[]{:S(2)}) async-start(), calls=%async_computation.4 | async-start | bytes 2621440 | tf_op jit(solution)/shard_map/all_gather | solution.py:51
Sparse Core Ops, SparseCore 0:
  31.6 27.6 reduce-scatter.1
  78.2 24.9 reduce-scatter.1
  122.0 24.9 reduce-scatter.1
  165.8 24.9 reduce-scatter.1
  209.6 24.9 reduce-scatter.1
  253.4 24.9 reduce-scatter.1
  297.2 24.9 reduce-scatter.1
  341.0 24.9 reduce-scatter.1
  384.8 24.9 reduce-scatter.1
  428.7 24.9 reduce-scatter.1
  492.9 21.1 all-gather.1
Sparse Core Ops, SparseCore 1:
  472.5 54.1 all-reduce.2
